TPU v7x, 128 devices: a whole 4x4x4 slice. The times are simulated.
128 devices in a mesh: lat: 2 (over core), lon: 8 (over y, x_hi), lev: 8 (over z, x_lo).
Axes of the slice: x: 4 (x_hi: 2, x_lo: 2; x = x_hi * 2 + x_lo), y: 4, z: 4, core: 2. Of those that a mesh axis runs over, the one named last changes fastest.
Arguments:
- field_values: float32 [16, 1024, 128, 128], P('lat', 'lon', 'lev'), may hold values from 0.2 to 1.8
- crowding: float32 [16, 1024, 128, 128], P('lat', 'lon', 'lev'), may hold values from 0.5 to 2
Outputs:
- potential: float32 [16, 1024, 128, 128], P('lat', 'lon', 'lev')
- field_values_end: float32 [16, 1024, 128, 128], P('lat', 'lon', 'lev')
All inputs are finite; a program needn't handle non-finite values.
Results may differ from a plain program's by a relative error of at most 0.00002.
Values sent between devices are 32-bit elements; how exact they have to be, the bound alone decides.
A program may use at most 256 MiB of HBM per device.

v0:
```python
import functools

import jax
import jax.numpy as jnp
from jax import lax
from jax.experimental import pallas as pl
from jax.experimental.pallas import tpu as pltpu
from jax.sharding import PartitionSpec as P

STEPS = 4
GROUP = 8
MESH = pl.DeviceIdType.MESH


def kernel(
    width, scale, field_hbm, crowd_hbm, pot, end,
    F, C, H, S, T, Q, R, X, B,
    ld_f, ld_c, z_send, z_recv, y_send, y_recv, x_send, x_recv, q_send, q_recv, b_send, b_recv,
):
    ny, nx, nz, _ = field_hbm.shape
    chunks = nx // width
    lat, lon, lev = (lax.axis_index(a) for a in ("lat", "lon", "lev"))
    n_lon, n_lev = lax.axis_size("lon"), lax.axis_size("lev")
    levels = n_lev // 2
    at_z, at_x = lax.div(lev, 2), lax.rem(lev, 2)
    up = (lat, lon, lax.rem(lev + 1, n_lev))
    down = (lat, lon, lax.rem(lev + n_lev - 1, n_lev))
    right = (lat, lax.rem(lon + 1, n_lon), lev)
    left = (lat, lax.rem(lon + n_lon - 1, n_lon), lev)
    core = (1 - lat, lon, lev)
    above = (lat, lon, lax.rem(lev + 2, n_lev))
    beneath = (lat, lon, lax.rem(lev + n_lev - 2, n_lev))
    partner = (lat, lon, lev + 1 - 2 * at_x)

    def load_field(c):
        columns = pl.ds(c * width, width)
        inside = pl.ds(c * width + 1, width)
        return pltpu.make_async_copy(
            field_hbm.at[:, columns], F.at[0, pl.ds(1, ny), inside], ld_f.at[c]
        )

    def load_crowding(c):
        columns = pl.ds(c * width, width)
        return pltpu.make_async_copy(crowd_hbm.at[:, columns], C.at[:, columns], ld_c.at[c])

    def in_turn(i):
        return lax.rem(i + (chunks - 1), chunks)

    def start_loads(i, carry):
        load_field(in_turn(i)).start()
        return carry

    lax.fori_loop(0, chunks, start_loads, 0)

    def start_crowding(i, carry):
        load_crowding(in_turn(i)).start()
        return carry

    lax.fori_loop(0, chunks, start_crowding, 0)

    @pl.when(at_z == 0)
    def _():
        def clear(c, carry):
            Q[c] = jnp.zeros(Q.shape[1:], Q.dtype)
            return carry

        lax.fori_loop(0, chunks, clear, 0)

    barrier = pltpu.get_barrier_semaphore()
    peers = (up, down, right, left, core, above, beneath)
    for peer in peers:
        pl.semaphore_signal(barrier, inc=1, device_id=peer, device_id_type=MESH)
    pl.semaphore_wait(barrier, len(peers))

    def remote(src, dst, send, recv, to):
        return pltpu.make_async_remote_copy(
            src_ref=src, dst_ref=dst, send_sem=send, recv_sem=recv, device_id=to, device_id_type=MESH
        )

    def faces(p, c):
        inside = pl.ds(c * width + 1, width)
        return (
            remote(S.at[p, 1, c], H.at[p, 0, c], z_send.at[p, 0, c], z_recv.at[p, 0, c], up),
            remote(S.at[p, 0, c], H.at[p, 1, c], z_send.at[p, 1, c], z_recv.at[p, 1, c], down),
            remote(F.at[p, ny, inside], F.at[p, 0, inside], y_send.at[p, 0, c], y_recv.at[p, 0, c], core),
            remote(F.at[p, 1, inside], F.at[p, ny + 1, inside], y_send.at[p, 1, c], y_recv.at[p, 1, c], core),
        )

    def right_face(p):
        rows = pl.ds(1, ny)
        return remote(F.at[p, rows, nx], F.at[p, rows, 0], x_send.at[p, 0], x_recv.at[p, 0], right)

    def left_face(p):
        rows = pl.ds(1, ny)
        return remote(F.at[p, rows, 1], F.at[p, rows, nx + 1], x_send.at[p, 1], x_recv.at[p, 1], left)

    def start_faces(p, c):
        @pl.when(c == chunks - 1)
        def _():
            right_face(p).start()

        @pl.when(c == 0)
        def _():
            left_face(p).start()

        for copy in faces(p, c):
            copy.start()

    def await_faces(p, c):
        for copy in faces(p, c):
            copy.wait_recv()

        @pl.when(c == 0)
        def _():
            right_face(p).wait_recv()

        @pl.when(c == chunks - 1)
        def _():
            left_face(p).wait_recv()

    def await_sent(p, c):
        for copy in faces(p, c):
            copy.wait_send()

        @pl.when(c == chunks - 1)
        def _():
            right_face(p).wait_send()

        @pl.when(c == 0)
        def _():
            left_face(p).wait_send()

    groups = width // GROUP

    def over_groups(c, body):
        def row(y, carry):
            def group(g, inner):
                body(y, g * GROUP, c * width + g * GROUP)
                return inner

            return lax.fori_loop(0, groups, group, carry)

        lax.fori_loop(0, ny, row, 0)

    def compute(step, c):
        p = step % 2
        level = lax.broadcasted_iota(jnp.int32, (nz, 128), 0)

        def body(y, g, x):
            columns = [F[p, y + 1, x + j] for j in range(GROUP + 2)]
            for j in range(GROUP):
                middle = columns[j + 1]
                low = H[p, 0, c, y, pl.ds(g + j, 1), :]
                high = H[p, 1, c, y, pl.ds(g + j, 1), :]
                under = jnp.where(level == 0, low, pltpu.roll(middle, 1, 0))
                over = jnp.where(level == nz - 1, high, pltpu.roll(middle, nz - 1, 0))
                total = columns[j] + columns[j + 2] + F[p, y, x + j + 1] + F[p, y + 2, x + j + 1] + under + over
                new = 0.1 * total + middle * (0.6 - 0.2 * (middle * C[y, x + j]))
                if step < STEPS - 1:
                    F[1 - p, y + 1, x + j + 1] = new
                    S[1 - p, 0, c, y, pl.ds(g + j, 1), :] = new[0:1]
                    S[1 - p, 1, c, y, pl.ds(g + j, 1), :] = new[nz - 1 : nz]
                else:
                    end[y, x + j] = new
                    here = new
                    reach = 1
                    while reach < nz:
                        here = here + jnp.where(level >= reach, pltpu.roll(here, reach, 0), 0.0)
                        reach *= 2
                    pot[y, x + j] = here * scale
                    T[c, y, pl.ds(g + j, 1), :] = here[nz - 1 : nz]

        over_groups(c, body)

    def first(i, carry):
        c = in_turn(i)
        load_field(c).wait()

        def body(y, g, x):
            for j in range(GROUP):
                value = F[0, y + 1, x + j + 1]
                S[0, 0, c, y, pl.ds(g + j, 1), :] = value[0:1]
                S[0, 1, c, y, pl.ds(g + j, 1), :] = value[nz - 1 : nz]

        over_groups(c, body)
        start_faces(0, c)
        return carry

    lax.fori_loop(0, chunks, first, 0)

    def upward(c):
        return remote(R.at[c], Q.at[c], q_send.at[c], q_recv.at[c], above)

    def across(c):
        return remote(X.at[c], B.at[c], b_send.at[c], b_recv.at[c], partner)

    def chain(c):
        @pl.when(at_z > 0)
        def _():
            upward(c).wait_recv()

        before = Q[c]
        through = before + T[c]
        R[c] = through
        X[c] = jnp.where(at_x == 0, through, before)

        @pl.when(at_z < levels - 1)
        def _():
            upward(c).start()

        across(c).start()

    for step in range(STEPS):
        p = step % 2

        def advance(i, carry):
            c = in_turn(i)
            if step == 0:
                load_crowding(c).wait()
            else:
                await_sent(1 - p, c)
            await_faces(p, c)
            compute(step, c)
            if step < STEPS - 1:
                start_faces(1 - p, c)
            else:
                chain(c)
            return carry

        lax.fori_loop(0, chunks, advance, 0)

    def finish(i, carry):
        c = in_turn(i)
        across(c).wait_recv()
        T[c] = (Q[c] + B[c]) * scale

        def body(y, g, x):
            for j in range(GROUP):
                pot[y, x + j] = pot[y, x + j] + T[c, y, pl.ds(g + j, 1), :]

        over_groups(c, body)
        return carry

    lax.fori_loop(0, chunks, finish, 0)

    def drain(i, carry):
        c = in_turn(i)
        await_sent((STEPS - 1) % 2, c)
        across(c).wait_send()

        @pl.when(at_z < levels - 1)
        def _():
            upward(c).wait_send()

        return carry

    lax.fori_loop(0, chunks, drain, 0)


def per_device(field_values, crowding):
    ny, nx, nz, lanes = field_values.shape
    width = min(16, nx // 2)
    chunks = nx // width
    scale = 1.0 / (nz * lax.axis_size("lev"))
    f32 = jnp.float32
    plane = (chunks, ny, width, lanes)
    dma = pltpu.SemaphoreType.DMA
    hbm = pl.BlockSpec(memory_space=pltpu.HBM)
    vmem = pl.BlockSpec(memory_space=pltpu.VMEM)
    return pl.pallas_call(
        functools.partial(kernel, width, scale),
        out_shape=(pltpu.VMEM(field_values.shape, f32), pltpu.VMEM(field_values.shape, f32)),
        in_specs=[hbm, hbm],
        out_specs=(vmem, vmem),
        scratch_shapes=[
            pltpu.VMEM((2, ny + 2, nx + 2, nz, lanes), f32),
            pltpu.VMEM(field_values.shape, f32),
            pltpu.VMEM((2, 2) + plane, f32),
            pltpu.VMEM((2, 2) + plane, f32),
            pltpu.VMEM(plane, f32),
            pltpu.VMEM(plane, f32),
            pltpu.VMEM(plane, f32),
            pltpu.VMEM(plane, f32),
            pltpu.VMEM(plane, f32),
            dma((chunks,)), dma((chunks,)),
            dma((2, 2, chunks)), dma((2, 2, chunks)),
            dma((2, 2, chunks)), dma((2, 2, chunks)),
            dma((2, 2)), dma((2, 2)),
            dma((chunks,)), dma((chunks,)),
            dma((chunks,)), dma((chunks,)),
        ],
        compiler_params=pltpu.CompilerParams(
            collective_id=0, has_side_effects=True, vmem_limit_bytes=42 * 2**20
        ),
    )(field_values, crowding)


def solution(mesh):
    spec = P("lat", "lon", "lev", None)
    return jax.shard_map(
        per_device, mesh=mesh, in_specs=(spec, spec), out_specs=(spec, spec), check_vma=False
    )
```

profile of v0, /device:TPU:102, one launch (start us, length us, event | category | flops | bytes accessed | tf_op | source)
XLA Modules:
  0.0 129.9 jit_solution(5906994645848484823)
XLA Ops:
  0.6 122.4 %shard_map.41 = (f32[8,128,16,128]{3,2,1,0:T(8,128)S(1)}, f32[8,128,16,128]{3,2,1,0:T(8,128)S(1)}) custom-call(f32[8,128,16,128]{3,2,1,0:T(8,128)} %field_hbm.1, f32[8,128,16,128]{3,2,1,0:T(8,128)} %crowd_hbm.1), custom_call_target="tpu_custom_call" | custom-call | tf_op jit(solution)/shard_map/pallas_call | solution.py:270
  123.1 3.4 %copy.6 = f32[8,128,16,128]{3,2,1,0:T(8,128)} copy(f32[8,128,16,128]{3,2,1,0:T(8,128)S(1)} %get-tuple-element.2) | data formatting | bytes 16777216
  126.5 3.4 %copy.7 = f32[8,128,16,128]{3,2,1,0:T(8,128)} copy(f32[8,128,16,128]{3,2,1,0:T(8,128)S(1)} %get-tuple-element.3) | data formatting | bytes 16777216
where the time goes:
time: 132 us; the launch traced here: 130 us
  Pallas kernels  122 us (92%)
  local copies, waits for them, and re-layouts  6.8 us (5%)
    pallas_call x1, Pallas kernels, per_device(): pl.pallas_call(functools.partial(kernel, width, scale), out_shape=(pltpu....  122 us
    unnamed x2, local copies, waits for them, and re-layouts  6.8 us

commit v1 on v0

--- a/solution.py
+++ b/solution.py
@@ -14,14 +14,15 @@
 
 def kernel(
     width, scale, field_hbm, crowd_hbm, pot, end,
-    F, C, H, S, T, Q, R, X, B,
-    ld_f, ld_c, z_send, z_recv, y_send, y_recv, x_send, x_recv, q_send, q_recv, b_send, b_recv,
+    F, C, H, S, T, Q, R, U, V, X, B,
+    met, ld_f, ld_c, z_send, z_recv, y_send, y_recv, x_send, x_recv, q_send, q_recv, b_send, b_recv,
 ):
     ny, nx, nz, _ = field_hbm.shape
     chunks = nx // width
+    ahead = chunks // 2
     lat, lon, lev = (lax.axis_index(a) for a in ("lat", "lon", "lev"))
     n_lon, n_lev = lax.axis_size("lon"), lax.axis_size("lev")
-    levels = n_lev // 2
+    assert n_lev == 8
     at_z, at_x = lax.div(lev, 2), lax.rem(lev, 2)
     up = (lat, lon, lax.rem(lev + 1, n_lev))
     down = (lat, lon, lax.rem(lev + n_lev - 1, n_lev))
@@ -32,6 +33,11 @@
     beneath = (lat, lon, lax.rem(lev + n_lev - 2, n_lev))
     partner = (lat, lon, lev + 1 - 2 * at_x)
 
+    barrier = pltpu.get_barrier_semaphore()
+    early = (down, left, core)
+    for peer in early:
+        pl.semaphore_signal(barrier, inc=1, device_id=peer, device_id_type=MESH)
+
     def load_field(c):
         columns = pl.ds(c * width, width)
         inside = pl.ds(c * width + 1, width)
@@ -57,20 +63,6 @@
         return carry
 
     lax.fori_loop(0, chunks, start_crowding, 0)
-
-    @pl.when(at_z == 0)
-    def _():
-        def clear(c, carry):
-            Q[c] = jnp.zeros(Q.shape[1:], Q.dtype)
-            return carry
-
-        lax.fori_loop(0, chunks, clear, 0)
-
-    barrier = pltpu.get_barrier_semaphore()
-    peers = (up, down, right, left, core, above, beneath)
-    for peer in peers:
-        pl.semaphore_signal(barrier, inc=1, device_id=peer, device_id_type=MESH)
-    pl.semaphore_wait(barrier, len(peers))
 
     def remote(src, dst, send, recv, to):
         return pltpu.make_async_remote_copy(
@@ -93,6 +85,21 @@
     def left_face(p):
         rows = pl.ds(1, ny)
         return remote(F.at[p, rows, 1], F.at[p, rows, nx + 1], x_send.at[p, 1], x_recv.at[p, 1], left)
+
+    def start_onward(p, c):
+        @pl.when(c == chunks - 1)
+        def _():
+            right_face(p).start()
+
+        for k in (0, 2, 3):
+            faces(p, c)[k].start()
+
+    def start_back(p, c):
+        @pl.when(c == 0)
+        def _():
+            left_face(p).start()
+
+        faces(p, c)[1].start()
 
     def start_faces(p, c):
         @pl.when(c == chunks - 1)
@@ -172,8 +179,7 @@
 
         over_groups(c, body)
 
-    def first(i, carry):
-        c = in_turn(i)
+    def prepare(c):
         load_field(c).wait()
 
         def body(y, g, x):
@@ -183,31 +189,87 @@
                 S[0, 1, c, y, pl.ds(g + j, 1), :] = value[nz - 1 : nz]
 
         over_groups(c, body)
+
+    prepare(in_turn(0))
+    pl.semaphore_wait(barrier, len(early))
+    pl.semaphore_signal(met.at[0], inc=1, device_id=up, device_id_type=MESH)
+    pl.semaphore_signal(met.at[1], inc=1, device_id=right, device_id_type=MESH)
+    start_onward(0, in_turn(0))
+
+    def first_onward(i, carry):
+        c = in_turn(i)
+        prepare(c)
+        start_onward(0, c)
+        return carry
+
+    def first_back(i, carry):
+        start_back(0, in_turn(i))
+        return carry
+
+    def first_both(i, carry):
+        c = in_turn(i)
+        prepare(c)
         start_faces(0, c)
         return carry
 
-    lax.fori_loop(0, chunks, first, 0)
-
-    def upward(c):
-        return remote(R.at[c], Q.at[c], q_send.at[c], q_recv.at[c], above)
+    lax.fori_loop(1, ahead, first_onward, 0)
+    pl.semaphore_wait(met.at[0], 1)
+    pl.semaphore_wait(met.at[1], 1)
+    lax.fori_loop(0, ahead, first_back, 0)
+    lax.fori_loop(ahead, chunks, first_both, 0)
+
+    def sent_on(src, dst, k, c, to):
+        return remote(src.at[c], dst.at[c], q_send.at[k, c], q_recv.at[k, c], to)
 
     def across(c):
         return remote(X.at[c], B.at[c], b_send.at[c], b_recv.at[c], partner)
 
-    def chain(c):
-        @pl.when(at_z > 0)
-        def _():
-            upward(c).wait_recv()
-
-        before = Q[c]
-        through = before + T[c]
-        R[c] = through
-        X[c] = jnp.where(at_x == 0, through, before)
-
-        @pl.when(at_z < levels - 1)
-        def _():
-            upward(c).start()
-
+    def chain_own(c):
+        @pl.when(at_z < 2)
+        def _():
+            sent_on(T, Q, 0, c, above).start()
+
+        @pl.when(at_z == 0)
+        def _():
+            sent_on(T, Q, 1, c, beneath).start()
+
+    def chain_first(c):
+        @pl.when(at_z == 1)
+        def _():
+            sent_on(T, Q, 0, c, above).wait_recv()
+
+        @pl.when(at_z == 2)
+        def _():
+            sent_on(T, Q, 0, c, above).wait_recv()
+            U[c] = Q[c] + T[c]
+            sent_on(U, R, 0, c, above).start()
+
+        @pl.when(at_z == 3)
+        def _():
+            sent_on(T, Q, 1, c, beneath).wait_recv()
+            sent_on(Q, R, 1, c, beneath).start()
+
+    def chain_second(c):
+        @pl.when(at_z == 0)
+        def _():
+            V[c] = jnp.zeros(V.shape[1:], V.dtype)
+
+        @pl.when(at_z == 1)
+        def _():
+            V[c] = Q[c]
+
+        @pl.when(at_z == 2)
+        def _():
+            sent_on(Q, R, 1, c, beneath).wait_recv()
+            V[c] = Q[c] + R[c]
+
+        @pl.when(at_z == 3)
+        def _():
+            sent_on(U, R, 0, c, above).wait_recv()
+            V[c] = Q[c] + R[c]
+
+        before = V[c]
+        X[c] = jnp.where(at_x == 0, before + T[c], before)
         across(c).start()
 
     for step in range(STEPS):
@@ -224,19 +286,32 @@
             if step < STEPS - 1:
                 start_faces(1 - p, c)
             else:
-                chain(c)
+                chain_own(c)
+
+                @pl.when(i >= 1)
+                def _():
+                    chain_first(in_turn(i - 1))
+
+                @pl.when(i >= 2)
+                def _():
+                    chain_second(in_turn(i - 2))
+
             return carry
 
         lax.fori_loop(0, chunks, advance, 0)
+
+    chain_first(in_turn(chunks - 1))
+    chain_second(in_turn(chunks - 2))
+    chain_second(in_turn(chunks - 1))
 
     def finish(i, carry):
         c = in_turn(i)
         across(c).wait_recv()
-        T[c] = (Q[c] + B[c]) * scale
+        V[c] = (V[c] + B[c]) * scale
 
         def body(y, g, x):
             for j in range(GROUP):
-                pot[y, x + j] = pot[y, x + j] + T[c, y, pl.ds(g + j, 1), :]
+                pot[y, x + j] = pot[y, x + j] + V[c, y, pl.ds(g + j, 1), :]
 
         over_groups(c, body)
         return carry
@@ -248,13 +323,31 @@
         await_sent((STEPS - 1) % 2, c)
         across(c).wait_send()
 
-        @pl.when(at_z < levels - 1)
-        def _():
-            upward(c).wait_send()
+        @pl.when(at_z != 3)
+        def _():
+            sent_on(T, Q, 0, c, above).wait_send()
+
+        @pl.when((at_z == 0) | (at_z == 3))
+        def _():
+            sent_on(T, Q, 1, c, beneath).wait_send()
 
         return carry
 
     lax.fori_loop(0, chunks, drain, 0)
+
+
+def put_out(pot, end, pot_out, end_out, sems):
+    pieces = sems.shape[1]
+    depth = pot.shape[0] // pieces
+    copies = [
+        pltpu.make_async_copy(src.at[pl.ds(k * depth, depth)], dst.at[pl.ds(k * depth, depth)], sems.at[i, k])
+        for k in range(pieces)
+        for i, (src, dst) in enumerate(((pot, pot_out), (end, end_out)))
+    ]
+    for copy in copies:
+        copy.start()
+    for copy in copies:
+        copy.wait()
 
 
 def per_device(field_values, crowding):
@@ -267,7 +360,7 @@
     dma = pltpu.SemaphoreType.DMA
     hbm = pl.BlockSpec(memory_space=pltpu.HBM)
     vmem = pl.BlockSpec(memory_space=pltpu.VMEM)
-    return pl.pallas_call(
+    results = pl.pallas_call(
         functools.partial(kernel, width, scale),
         out_shape=(pltpu.VMEM(field_values.shape, f32), pltpu.VMEM(field_values.shape, f32)),
         in_specs=[hbm, hbm],
@@ -282,17 +375,30 @@
             pltpu.VMEM(plane, f32),
             pltpu.VMEM(plane, f32),
             pltpu.VMEM(plane, f32),
+            pltpu.VMEM(plane, f32),
+            pltpu.VMEM(plane, f32),
+            pltpu.SemaphoreType.REGULAR((2,)),
             dma((chunks,)), dma((chunks,)),
             dma((2, 2, chunks)), dma((2, 2, chunks)),
             dma((2, 2, chunks)), dma((2, 2, chunks)),
             dma((2, 2)), dma((2, 2)),
-            dma((chunks,)), dma((chunks,)),
+            dma((2, chunks)), dma((2, chunks)),
             dma((chunks,)), dma((chunks,)),
         ],
         compiler_params=pltpu.CompilerParams(
             collective_id=0, has_side_effects=True, vmem_limit_bytes=42 * 2**20
         ),
     )(field_values, crowding)
+    shape = jax.ShapeDtypeStruct(field_values.shape, f32)
+    pieces = 4
+    return tuple(pl.pallas_call(
+        put_out,
+        out_shape=(shape, shape),
+        in_specs=[vmem, vmem],
+        out_specs=(hbm, hbm),
+        scratch_shapes=[dma((2, pieces))],
+        compiler_params=pltpu.CompilerParams(vmem_limit_bytes=2**20),
+    )(*results))
 
 
 def solution(mesh):

time: 132 us -> 127 us (0.962)
  local copies, waits for them, and re-layouts: 6.8 us -> 0 us
  Pallas kernels: 122 us -> 124 us
    unnamed x2 -> x0, local copies, waits for them, and re-layouts: 6.8 us -> none
    pallas_call x0 -> x1, Pallas kernels: none -> 5.92 us  [per_device(): pl.pallas_call(put_out, out_shape=(shape, shape), in_specs=[vmem, vmem],...]
    pallas_call x1, Pallas kernels: 122 us -> 118 us  [per_device(): pl.pallas_call(functools.partial(kernel, width, scale), out_shape=(pltpu....]
where the time goes in v1:
time: 127 us; the launch traced here: 125 us
  Pallas kernels  124 us (98%)
    pallas_call x1, Pallas kernels, per_device(): pl.pallas_call(functools.partial(kernel, width, scale), out_shape=(pltpu....  118 us
    pallas_call x1, Pallas kernels, per_device(): pl.pallas_call(put_out, out_shape=(shape, shape), in_specs=[vmem, vmem],...  5.92 us

profile of v1, /device:TPU:102, one launch (start us, length us, event | category | flops | bytes accessed | tf_op | source)
XLA Modules:
  0.0 124.8 jit_solution(5238067418661888537)
XLA Ops:
  0.6 118.2 %shard_map.41 = (f32[8,128,16,128]{3,2,1,0:T(8,128)S(1)}, f32[8,128,16,128]{3,2,1,0:T(8,128)S(1)}) custom-call(f32[8,128,16,128]{3,2,1,0:T(8,128)} %field_hbm.1, f32[8,128,16,128]{3,2,1,0:T(8,128)} %crowd_hbm.1), custom_call_target="tpu_custom_call" | custom-call | tf_op jit(solution)/shard_map/pallas_call | solution.py:363
  118.9 5.9 %shard_map.42 = (f32[8,128,16,128]{3,2,1,0:T(8,128)}, f32[8,128,16,128]{3,2,1,0:T(8,128)}) custom-call(f32[8,128,16,128]{3,2,1,0:T(8,128)S(1)} %get-tuple-element.4.pot, f32[8,128,16,128]{3,2,1,0:T(8,128)S(1)} %get-tuple-element.5.end), custom_call_target="tpu_custom_call" | custom-call | tf_op jit(solution)/shard_map/pallas_call | solution.py:394

commit v2 on v1

--- a/solution.py
+++ b/solution.py
@@ -9,17 +9,19 @@
 
 STEPS = 4
 GROUP = 8
+LAG = 4
 MESH = pl.DeviceIdType.MESH
 
 
 def kernel(
     width, scale, field_hbm, crowd_hbm, pot, end,
     F, C, H, S, T, Q, R, U, V, X, B,
-    met, ld_f, ld_c, z_send, z_recv, y_send, y_recv, x_send, x_recv, q_send, q_recv, b_send, b_recv,
+    met, ld, f_send, f_recv, x_recv, q_send, q_recv, b_send, b_recv,
 ):
     ny, nx, nz, _ = field_hbm.shape
     chunks = nx // width
     ahead = chunks // 2
+    lag = LAG
     lat, lon, lev = (lax.axis_index(a) for a in ("lat", "lon", "lev"))
     n_lon, n_lev = lax.axis_size("lon"), lax.axis_size("lev")
     assert n_lev == 8
@@ -38,31 +40,30 @@
     for peer in early:
         pl.semaphore_signal(barrier, inc=1, device_id=peer, device_id_type=MESH)
 
-    def load_field(c):
-        columns = pl.ds(c * width, width)
-        inside = pl.ds(c * width + 1, width)
-        return pltpu.make_async_copy(
-            field_hbm.at[:, columns], F.at[0, pl.ds(1, ny), inside], ld_f.at[c]
-        )
-
-    def load_crowding(c):
-        columns = pl.ds(c * width, width)
-        return pltpu.make_async_copy(crowd_hbm.at[:, columns], C.at[:, columns], ld_c.at[c])
-
     def in_turn(i):
         return lax.rem(i + (chunks - 1), chunks)
 
-    def start_loads(i, carry):
-        load_field(in_turn(i)).start()
-        return carry
-
-    lax.fori_loop(0, chunks, start_loads, 0)
-
-    def start_crowding(i, carry):
-        load_crowding(in_turn(i)).start()
-        return carry
-
-    lax.fori_loop(0, chunks, start_crowding, 0)
+    def load_field(k):
+        start, stop = ((nx - width, nx), (0, width), (width, nx - width))[k]
+        return pltpu.make_async_copy(
+            field_hbm.at[:, start:stop], F.at[0, 1 : ny + 1, start + 1 : stop + 1], ld.at[k]
+        )
+
+    def load_crowding():
+        return pltpu.make_async_copy(crowd_hbm, C, ld.at[3])
+
+    for k in range(3):
+        load_field(k).start()
+    load_crowding().start()
+
+    def arrived(rows, sem):
+        columns = rows // nz
+        deep = max(k for k in range(1, ny + 1) if columns % k == 0 and columns // k <= nx)
+        part = F.at[0, :deep, : columns // deep]
+        return pltpu.make_async_copy(part, part, sem)
+
+    chunk_rows = 2 * width * (ny + nz)
+    step_rows = chunks * chunk_rows + 2 * ny * nz
 
     def remote(src, dst, send, recv, to):
         return pltpu.make_async_remote_copy(
@@ -71,71 +72,52 @@
 
     def faces(p, c):
         inside = pl.ds(c * width + 1, width)
+        sems = (f_send.at[p], f_recv.at[p, c])
         return (
-            remote(S.at[p, 1, c], H.at[p, 0, c], z_send.at[p, 0, c], z_recv.at[p, 0, c], up),
-            remote(S.at[p, 0, c], H.at[p, 1, c], z_send.at[p, 1, c], z_recv.at[p, 1, c], down),
-            remote(F.at[p, ny, inside], F.at[p, 0, inside], y_send.at[p, 0, c], y_recv.at[p, 0, c], core),
-            remote(F.at[p, 1, inside], F.at[p, ny + 1, inside], y_send.at[p, 1, c], y_recv.at[p, 1, c], core),
+            remote(S.at[p, 1, c], H.at[p, 0, c], *sems, up),
+            remote(S.at[p, 0, c], H.at[p, 1, c], *sems, down),
+            remote(F.at[p, ny, inside], F.at[p, 0, inside], *sems, core),
+            remote(F.at[p, 1, inside], F.at[p, ny + 1, inside], *sems, core),
         )
 
     def right_face(p):
         rows = pl.ds(1, ny)
-        return remote(F.at[p, rows, nx], F.at[p, rows, 0], x_send.at[p, 0], x_recv.at[p, 0], right)
+        return remote(F.at[p, rows, nx], F.at[p, rows, 0], f_send.at[p], x_recv.at[p, 0], right)
 
     def left_face(p):
         rows = pl.ds(1, ny)
-        return remote(F.at[p, rows, 1], F.at[p, rows, nx + 1], x_send.at[p, 1], x_recv.at[p, 1], left)
-
-    def start_onward(p, c):
+        return remote(F.at[p, rows, 1], F.at[p, rows, nx + 1], f_send.at[p], x_recv.at[p, 1], left)
+
+    def start_faces(p, c, onward=True, back=True):
+        if onward:
+
+            @pl.when(c == chunks - 1)
+            def _():
+                right_face(p).start()
+
+        if back:
+
+            @pl.when(c == 0)
+            def _():
+                left_face(p).start()
+
+        ahead_up, ahead_down, upper, lower = faces(p, c)
+        for copy in onward * (ahead_up, upper, lower) + back * (ahead_down,):
+            copy.start()
+
+    def await_faces(p, c):
+        arrived(chunk_rows, f_recv.at[p, c]).wait()
+
+        @pl.when(c == 0)
+        def _():
+            right_face(p).wait_recv()
+
         @pl.when(c == chunks - 1)
         def _():
-            right_face(p).start()
-
-        for k in (0, 2, 3):
-            faces(p, c)[k].start()
-
-    def start_back(p, c):
-        @pl.when(c == 0)
-        def _():
-            left_face(p).start()
-
-        faces(p, c)[1].start()
-
-    def start_faces(p, c):
-        @pl.when(c == chunks - 1)
-        def _():
-            right_face(p).start()
-
-        @pl.when(c == 0)
-        def _():
-            left_face(p).start()
-
-        for copy in faces(p, c):
-            copy.start()
-
-    def await_faces(p, c):
-        for copy in faces(p, c):
-            copy.wait_recv()
-
-        @pl.when(c == 0)
-        def _():
-            right_face(p).wait_recv()
-
-        @pl.when(c == chunks - 1)
-        def _():
             left_face(p).wait_recv()
 
-    def await_sent(p, c):
-        for copy in faces(p, c):
-            copy.wait_send()
-
-        @pl.when(c == chunks - 1)
-        def _():
-            right_face(p).wait_send()
-
-        @pl.when(c == 0)
-        def _():
-            left_face(p).wait_send()
+    def await_sent(p):
+        arrived(step_rows, f_send.at[p]).wait()
 
     groups = width // GROUP
 
@@ -180,8 +162,6 @@
         over_groups(c, body)
 
     def prepare(c):
-        load_field(c).wait()
-
         def body(y, g, x):
             for j in range(GROUP):
                 value = F[0, y + 1, x + j + 1]
@@ -190,24 +170,27 @@
 
         over_groups(c, body)
 
-    prepare(in_turn(0))
+    load_field(0).wait()
+    prepare(chunks - 1)
     pl.semaphore_wait(barrier, len(early))
     pl.semaphore_signal(met.at[0], inc=1, device_id=up, device_id_type=MESH)
     pl.semaphore_signal(met.at[1], inc=1, device_id=right, device_id_type=MESH)
-    start_onward(0, in_turn(0))
-
-    def first_onward(i, carry):
-        c = in_turn(i)
+    start_faces(0, chunks - 1, back=False)
+    load_field(1).wait()
+    prepare(0)
+    start_faces(0, 0, back=False)
+    load_field(2).wait()
+
+    def first_onward(c, carry):
         prepare(c)
-        start_onward(0, c)
-        return carry
-
-    def first_back(i, carry):
-        start_back(0, in_turn(i))
-        return carry
-
-    def first_both(i, carry):
-        c = in_turn(i)
+        start_faces(0, c, back=False)
+        return carry
+
+    def first_back(c, carry):
+        start_faces(0, c, onward=False)
+        return carry
+
+    def first_both(c, carry):
         prepare(c)
         start_faces(0, c)
         return carry
@@ -215,14 +198,15 @@
     lax.fori_loop(1, ahead, first_onward, 0)
     pl.semaphore_wait(met.at[0], 1)
     pl.semaphore_wait(met.at[1], 1)
+    start_faces(0, chunks - 1, onward=False)
     lax.fori_loop(0, ahead, first_back, 0)
-    lax.fori_loop(ahead, chunks, first_both, 0)
+    lax.fori_loop(ahead, chunks - 1, first_both, 0)
 
     def sent_on(src, dst, k, c, to):
-        return remote(src.at[c], dst.at[c], q_send.at[k, c], q_recv.at[k, c], to)
+        return remote(src.at[c], dst.at[c], q_send.at[k], q_recv.at[k, c], to)
 
     def across(c):
-        return remote(X.at[c], B.at[c], b_send.at[c], b_recv.at[c], partner)
+        return remote(X.at[c], B.at[c], b_send, b_recv.at[c], partner)
 
     def chain_own(c):
         @pl.when(at_z < 2)
@@ -274,13 +258,13 @@
 
     for step in range(STEPS):
         p = step % 2
+        if step == 0:
+            load_crowding().wait()
+        else:
+            await_sent(1 - p)
 
         def advance(i, carry):
             c = in_turn(i)
-            if step == 0:
-                load_crowding(c).wait()
-            else:
-                await_sent(1 - p, c)
             await_faces(p, c)
             compute(step, c)
             if step < STEPS - 1:
@@ -288,21 +272,28 @@
             else:
                 chain_own(c)
 
-                @pl.when(i >= 1)
+                @pl.when(i >= lag)
                 def _():
-                    chain_first(in_turn(i - 1))
-
-                @pl.when(i >= 2)
+                    chain_first(in_turn(i - lag))
+
+                @pl.when(i >= 2 * lag)
                 def _():
-                    chain_second(in_turn(i - 2))
+                    chain_second(in_turn(i - 2 * lag))
 
             return carry
 
         lax.fori_loop(0, chunks, advance, 0)
 
-    chain_first(in_turn(chunks - 1))
-    chain_second(in_turn(chunks - 2))
-    chain_second(in_turn(chunks - 1))
+    def last_first(i, carry):
+        chain_first(in_turn(i))
+        return carry
+
+    def last_second(i, carry):
+        chain_second(in_turn(i))
+        return carry
+
+    lax.fori_loop(chunks - lag, chunks, last_first, 0)
+    lax.fori_loop(chunks - 2 * lag, chunks, last_second, 0)
 
     def finish(i, carry):
         c = in_turn(i)
@@ -318,22 +309,16 @@
 
     lax.fori_loop(0, chunks, finish, 0)
 
-    def drain(i, carry):
-        c = in_turn(i)
-        await_sent((STEPS - 1) % 2, c)
-        across(c).wait_send()
-
-        @pl.when(at_z != 3)
-        def _():
-            sent_on(T, Q, 0, c, above).wait_send()
-
-        @pl.when((at_z == 0) | (at_z == 3))
-        def _():
-            sent_on(T, Q, 1, c, beneath).wait_send()
-
-        return carry
-
-    lax.fori_loop(0, chunks, drain, 0)
+    await_sent((STEPS - 1) % 2)
+    pltpu.make_async_copy(X, X, b_send).wait()
+
+    @pl.when(at_z != 3)
+    def _():
+        pltpu.make_async_copy(T, T, q_send.at[0]).wait()
+
+    @pl.when((at_z == 0) | (at_z == 3))
+    def _():
+        pltpu.make_async_copy(T, T, q_send.at[1]).wait()
 
 
 def put_out(pot, end, pot_out, end_out, sems):
@@ -352,7 +337,7 @@
 
 def per_device(field_values, crowding):
     ny, nx, nz, lanes = field_values.shape
-    width = min(16, nx // 2)
+    width = 8
     chunks = nx // width
     scale = 1.0 / (nz * lax.axis_size("lev"))
     f32 = jnp.float32
@@ -378,12 +363,10 @@
             pltpu.VMEM(plane, f32),
             pltpu.VMEM(plane, f32),
             pltpu.SemaphoreType.REGULAR((2,)),
-            dma((chunks,)), dma((chunks,)),
-            dma((2, 2, chunks)), dma((2, 2, chunks)),
-            dma((2, 2, chunks)), dma((2, 2, chunks)),
-            dma((2, 2)), dma((2, 2)),
-            dma((2, chunks)), dma((2, chunks)),
-            dma((chunks,)), dma((chunks,)),
+            dma((4,)),
+            dma((2,)), dma((2, chunks)), dma((2, 2)),
+            dma((2,)), dma((2, chunks)),
+            dma, dma((chunks,)),
         ],
         compiler_params=pltpu.CompilerParams(
             collective_id=0, has_side_effects=True, vmem_limit_bytes=42 * 2**20

time: 127 us -> 125 us (0.984)
    pallas_call x1, Pallas kernels: 118 us -> 117 us  [per_device(): pl.pallas_call(functools.partial(kernel, width, scale), out_shape=(pltpu....]
where the time goes in v2:
time: 125 us; the launch traced here: 124 us
  Pallas kernels  123 us (98%)
    pallas_call x1, Pallas kernels, per_device(): pl.pallas_call(functools.partial(kernel, width, scale), out_shape=(pltpu....  117 us
    pallas_call x1, Pallas kernels, per_device(): pl.pallas_call(put_out, out_shape=(shape, shape), in_specs=[vmem, vmem],...  5.92 us

profile of v2, /device:TPU:102, one launch (start us, length us, event | category | flops | bytes accessed | tf_op | source)
XLA Modules:
  0.0 123.5 jit_solution(16117935602616470044)
XLA Ops:
  0.6 116.9 %shard_map.41 = (f32[8,128,16,128]{3,2,1,0:T(8,128)S(1)}, f32[8,128,16,128]{3,2,1,0:T(8,128)S(1)}) custom-call(f32[8,128,16,128]{3,2,1,0:T(8,128)} %field_hbm.1, f32[8,128,16,128]{3,2,1,0:T(8,128)} %crowd_hbm.1), custom_call_target="tpu_custom_call" | custom-call | tf_op jit(solution)/shard_map/pallas_call | solution.py:348
  117.6 5.9 %shard_map.42 = (f32[8,128,16,128]{3,2,1,0:T(8,128)}, f32[8,128,16,128]{3,2,1,0:T(8,128)}) custom-call(f32[8,128,16,128]{3,2,1,0:T(8,128)S(1)} %get-tuple-element.4.pot, f32[8,128,16,128]{3,2,1,0:T(8,128)S(1)} %get-tuple-element.5.end), custom_call_target="tpu_custom_call" | custom-call | tf_op jit(solution)/shard_map/pallas_call | solution.py:377

commit v3 on v2

--- a/solution.py
+++ b/solution.py
@@ -9,19 +9,23 @@
 
 STEPS = 4
 GROUP = 8
-LAG = 4
+FIRST = 2
+SECOND = 5
+LATE = 5
+DIRECT = 3
 MESH = pl.DeviceIdType.MESH
 
 
 def kernel(
-    width, scale, field_hbm, crowd_hbm, pot, end,
+    width, scale, field_hbm, crowd_hbm, pot, end, VL, XL,
     F, C, H, S, T, Q, R, U, V, X, B,
-    met, ld, f_send, f_recv, x_recv, q_send, q_recv, b_send, b_recv,
+    met, ld, f_send, f_recv, x_recv, q_send, q_recv, b_send,
 ):
     ny, nx, nz, _ = field_hbm.shape
     chunks = nx // width
     ahead = chunks // 2
-    lag = LAG
+    late_from = chunks - 1 - LATE
+    direct_from = chunks - 1 - DIRECT
     lat, lon, lev = (lax.axis_index(a) for a in ("lat", "lon", "lev"))
     n_lon, n_lev = lax.axis_size("lon"), lax.axis_size("lev")
     assert n_lev == 8
@@ -31,14 +35,25 @@
     right = (lat, lax.rem(lon + 1, n_lon), lev)
     left = (lat, lax.rem(lon + n_lon - 1, n_lon), lev)
     core = (1 - lat, lon, lev)
+    opposite = (lat, lon, lax.rem(lev + n_lev // 2, n_lev))
     above = (lat, lon, lax.rem(lev + 2, n_lev))
     beneath = (lat, lon, lax.rem(lev + n_lev - 2, n_lev))
     partner = (lat, lon, lev + 1 - 2 * at_x)
 
     barrier = pltpu.get_barrier_semaphore()
-    early = (down, left, core)
-    for peer in early:
-        pl.semaphore_signal(barrier, inc=1, device_id=peer, device_id_type=MESH)
+    odd = lax.rem(lon, 2)
+
+    def signal(sem, to):
+        pl.semaphore_signal(sem, inc=1, device_id=to, device_id_type=MESH)
+
+    signal(barrier, down)
+    signal(barrier, core)
+
+    @pl.when(odd == 0)
+    def _():
+        signal(barrier, right)
+        signal(barrier, left)
+
 
     def in_turn(i):
         return lax.rem(i + (chunks - 1), chunks)
@@ -54,7 +69,6 @@
 
     for k in range(3):
         load_field(k).start()
-    load_crowding().start()
 
     def arrived(rows, sem):
         columns = rows // nz
@@ -88,14 +102,12 @@
         rows = pl.ds(1, ny)
         return remote(F.at[p, rows, 1], F.at[p, rows, nx + 1], f_send.at[p], x_recv.at[p, 1], left)
 
-    def start_faces(p, c, onward=True, back=True):
-        if onward:
+    def start_faces(p, c, onward=True, back=True, columns=True):
+        if columns:
 
             @pl.when(c == chunks - 1)
             def _():
                 right_face(p).start()
-
-        if back:
 
             @pl.when(c == 0)
             def _():
@@ -172,41 +184,74 @@
 
     load_field(0).wait()
     prepare(chunks - 1)
-    pl.semaphore_wait(barrier, len(early))
-    pl.semaphore_signal(met.at[0], inc=1, device_id=up, device_id_type=MESH)
-    pl.semaphore_signal(met.at[1], inc=1, device_id=right, device_id_type=MESH)
-    start_faces(0, chunks - 1, back=False)
+    pl.semaphore_wait(barrier, 2 + 2 * odd)
+    signal(met.at[0], up)
+
+    @pl.when(odd == 1)
+    def _():
+        signal(met.at[1], left)
+        signal(met.at[2], right)
+
+    start_faces(0, chunks - 1, back=False, columns=False)
     load_field(1).wait()
     prepare(0)
-    start_faces(0, 0, back=False)
+    start_faces(0, 0, back=False, columns=False)
     load_field(2).wait()
 
     def first_onward(c, carry):
         prepare(c)
-        start_faces(0, c, back=False)
+        start_faces(0, c, back=False, columns=False)
         return carry
 
     def first_back(c, carry):
-        start_faces(0, c, onward=False)
+        start_faces(0, c, onward=False, columns=False)
         return carry
 
     def first_both(c, carry):
         prepare(c)
-        start_faces(0, c)
+        start_faces(0, c, columns=False)
         return carry
 
     lax.fori_loop(1, ahead, first_onward, 0)
+
+    @pl.when(odd == 0)
+    def _():
+        pl.semaphore_wait(met.at[1], 1)
+        pl.semaphore_wait(met.at[2], 1)
+
+    right_face(0).start()
+    left_face(0).start()
     pl.semaphore_wait(met.at[0], 1)
-    pl.semaphore_wait(met.at[1], 1)
-    start_faces(0, chunks - 1, onward=False)
+    start_faces(0, chunks - 1, onward=False, columns=False)
     lax.fori_loop(0, ahead, first_back, 0)
     lax.fori_loop(ahead, chunks - 1, first_both, 0)
+    load_crowding().start()
 
     def sent_on(src, dst, k, c, to):
         return remote(src.at[c], dst.at[c], q_send.at[k], q_recv.at[k, c], to)
 
     def across(c):
-        return remote(X.at[c], B.at[c], b_send, b_recv.at[c], partner)
+        return remote(X.at[c], B.at[c], b_send, f_recv.at[0, c], partner)
+
+    def pass_across(c, before):
+        onward = jnp.where(at_x == 0, before + T[c], before)
+
+        @pl.when((c < late_from) | (c == chunks - 1))
+        def _():
+            V[c] = before
+            X[c] = onward
+            across(c).start()
+
+        @pl.when((c >= late_from) & (c < chunks - 1))
+        def _():
+            VL[c - late_from] = before
+            XL[c - late_from] = onward
+
+    def goes_direct(c):
+        return (c >= direct_from) & (c < chunks - 1)
+
+    def direct(c):
+        return remote(T.at[c], R.at[c], q_send.at[1], q_recv.at[1, c], opposite)
 
     def chain_own(c):
         @pl.when(at_z < 2)
@@ -215,12 +260,19 @@
 
         @pl.when(at_z == 0)
         def _():
+
+            @pl.when(goes_direct(c))
+            def _():
+                direct(c).start()
+
             sent_on(T, Q, 1, c, beneath).start()
+            pass_across(c, jnp.zeros(V.shape[1:], V.dtype))
 
     def chain_first(c):
         @pl.when(at_z == 1)
         def _():
             sent_on(T, Q, 0, c, above).wait_recv()
+            pass_across(c, Q[c])
 
         @pl.when(at_z == 2)
         def _():
@@ -231,30 +283,22 @@
         @pl.when(at_z == 3)
         def _():
             sent_on(T, Q, 1, c, beneath).wait_recv()
-            sent_on(Q, R, 1, c, beneath).start()
+
+            @pl.when(jnp.logical_not(goes_direct(c)))
+            def _():
+                sent_on(Q, R, 1, c, beneath).start()
+
 
     def chain_second(c):
-        @pl.when(at_z == 0)
-        def _():
-            V[c] = jnp.zeros(V.shape[1:], V.dtype)
-
-        @pl.when(at_z == 1)
-        def _():
-            V[c] = Q[c]
-
         @pl.when(at_z == 2)
         def _():
             sent_on(Q, R, 1, c, beneath).wait_recv()
-            V[c] = Q[c] + R[c]
+            pass_across(c, Q[c] + R[c])
 
         @pl.when(at_z == 3)
         def _():
             sent_on(U, R, 0, c, above).wait_recv()
-            V[c] = Q[c] + R[c]
-
-        before = V[c]
-        X[c] = jnp.where(at_x == 0, before + T[c], before)
-        across(c).start()
+            pass_across(c, Q[c] + R[c])
 
     for step in range(STEPS):
         p = step % 2
@@ -272,13 +316,13 @@
             else:
                 chain_own(c)
 
-                @pl.when(i >= lag)
+                @pl.when(i >= FIRST)
                 def _():
-                    chain_first(in_turn(i - lag))
-
-                @pl.when(i >= 2 * lag)
+                    chain_first(in_turn(i - FIRST))
+
+                @pl.when(i >= SECOND)
                 def _():
-                    chain_second(in_turn(i - 2 * lag))
+                    chain_second(in_turn(i - SECOND))
 
             return carry
 
@@ -292,8 +336,8 @@
         chain_second(in_turn(i))
         return carry
 
-    lax.fori_loop(chunks - lag, chunks, last_first, 0)
-    lax.fori_loop(chunks - 2 * lag, chunks, last_second, 0)
+    lax.fori_loop(chunks - FIRST, chunks, last_first, 0)
+    lax.fori_loop(chunks - SECOND, chunks, last_second, 0)
 
     def finish(i, carry):
         c = in_turn(i)
@@ -307,30 +351,59 @@
         over_groups(c, body)
         return carry
 
-    lax.fori_loop(0, chunks, finish, 0)
+    lax.fori_loop(0, chunks - LATE, finish, 0)
 
     await_sent((STEPS - 1) % 2)
-    pltpu.make_async_copy(X, X, b_send).wait()
+    sent = X.at[: chunks - LATE]
+    pltpu.make_async_copy(sent, sent, b_send).wait()
 
     @pl.when(at_z != 3)
     def _():
         pltpu.make_async_copy(T, T, q_send.at[0]).wait()
 
-    @pl.when((at_z == 0) | (at_z == 3))
-    def _():
-        pltpu.make_async_copy(T, T, q_send.at[1]).wait()
-
-
-def put_out(pot, end, pot_out, end_out, sems):
-    pieces = sems.shape[1]
-    depth = pot.shape[0] // pieces
-    copies = [
-        pltpu.make_async_copy(src.at[pl.ds(k * depth, depth)], dst.at[pl.ds(k * depth, depth)], sems.at[i, k])
-        for k in range(pieces)
-        for i, (src, dst) in enumerate(((pot, pot_out), (end, end_out)))
-    ]
+    @pl.when(at_z == 0)
+    def _():
+        arrived((chunks + DIRECT) * ny * width, q_send.at[1]).wait()
+
+    @pl.when(at_z == 3)
+    def _():
+        arrived((chunks - DIRECT) * ny * width, q_send.at[1]).wait()
+
+
+def put_first(first, stop, pot, end, pot_out, end_out, sems):
+    half = pot.shape[0] // 2
+    nx = pot.shape[1]
+    copies = []
+    for k in range(2):
+        rows = pl.ds(k * half, half)
+        for src, dst, at in (
+            (end, end_out, slice(None)),
+            (pot, pot_out, slice(0, first)),
+            (pot, pot_out, slice(stop, nx)),
+        ):
+            copies.append(pltpu.make_async_copy(src.at[rows, at], dst.at[rows, at], sems.at[len(copies)]))
     for copy in copies:
         copy.start()
+    for copy in copies:
+        copy.wait()
+
+
+def put_late(first, width, scale, pot, VL, BL, pot_in, pot_out, held, sems):
+    del pot_in
+    ny = pot.shape[0]
+    copies = []
+    for k in range(LATE):
+        def row(y, carry, k=k):
+            below = (VL[k, y] + BL[k, y]) * scale
+            for j in range(width):
+                held[k, y, j] = pot[y, first + k * width + j] + below[j : j + 1]
+            return carry
+
+        lax.fori_loop(0, ny, row, 0)
+        copies.append(
+            pltpu.make_async_copy(held.at[k], pot_out.at[:, first + k * width : first + (k + 1) * width], sems.at[k])
+        )
+        copies[-1].start()
     for copy in copies:
         copy.wait()
 
@@ -347,9 +420,9 @@
     vmem = pl.BlockSpec(memory_space=pltpu.VMEM)
     results = pl.pallas_call(
         functools.partial(kernel, width, scale),
-        out_shape=(pltpu.VMEM(field_values.shape, f32), pltpu.VMEM(field_values.shape, f32)),
+        out_shape=(pltpu.VMEM(field_values.shape, f32),) * 2 + (pltpu.VMEM((LATE,) + plane[1:], f32),) * 2,
         in_specs=[hbm, hbm],
-        out_specs=(vmem, vmem),
+        out_specs=(vmem,) * 4,
         scratch_shapes=[
             pltpu.VMEM((2, ny + 2, nx + 2, nz, lanes), f32),
             pltpu.VMEM(field_values.shape, f32),
@@ -362,26 +435,41 @@
             pltpu.VMEM(plane, f32),
             pltpu.VMEM(plane, f32),
             pltpu.VMEM(plane, f32),
-            pltpu.SemaphoreType.REGULAR((2,)),
+            pltpu.SemaphoreType.REGULAR((3,)),
             dma((4,)),
             dma((2,)), dma((2, chunks)), dma((2, 2)),
             dma((2,)), dma((2, chunks)),
-            dma, dma((chunks,)),
+            dma,
         ],
         compiler_params=pltpu.CompilerParams(
             collective_id=0, has_side_effects=True, vmem_limit_bytes=42 * 2**20
         ),
     )(field_values, crowding)
+    pot, end, before, onward = results
     shape = jax.ShapeDtypeStruct(field_values.shape, f32)
-    pieces = 4
-    return tuple(pl.pallas_call(
-        put_out,
+    n_lev = lax.axis_size("lev")
+    first, stop = nx - width * (LATE + 1), nx - width
+    across = lax.ppermute(onward, "lev", [(k, k ^ 1) for k in range(n_lev)])
+    size = 4 * field_values.size
+    pot_out, end_out = pl.pallas_call(
+        functools.partial(put_first, first, stop),
         out_shape=(shape, shape),
         in_specs=[vmem, vmem],
         out_specs=(hbm, hbm),
-        scratch_shapes=[dma((2, pieces))],
+        scratch_shapes=[dma((6,))],
+        cost_estimate=pl.CostEstimate(flops=0, bytes_accessed=2 * size, transcendentals=0),
         compiler_params=pltpu.CompilerParams(vmem_limit_bytes=2**20),
-    )(*results))
+    )(pot, end)
+    pot_out = pl.pallas_call(
+        functools.partial(put_late, first, width, scale),
+        out_shape=shape,
+        in_specs=[vmem, vmem, vmem, hbm],
+        out_specs=hbm,
+        scratch_shapes=[pltpu.VMEM((LATE, ny, width, nz, lanes), f32), dma((LATE,))],
+        input_output_aliases={3: 0},
+        compiler_params=pltpu.CompilerParams(vmem_limit_bytes=4 * 2**20),
+    )(pot, before, across, pot_out)
+    return pot_out, end_out
 
 
 def solution(mesh):

time: 125 us -> 123 us (0.984); the launches traced: 124 us -> 123 us
  Pallas kernels: 123 us -> 121 us
  starting transfers between devices: 0 us -> 1.6 us
    pallas_call x1, Pallas kernels: 117 us -> 114 us  [per_device(): pl.pallas_call(functools.partial(kernel, width, scale), out_shape=(pltpu....]
    ppermute x0 -> x1, starting transfers between devices: none -> 1.6 us  [per_device(): across = lax.ppermute(onward, 'lev', [(k, k ^ 1) for k in range(n_lev)])]
    pallas_call x1 -> x2, Pallas kernels: 5.92 us -> 6.67 us  [the longest x1 5.05 us: per_device(): pl.pallas_call(functools.partial(put_first, first, stop), out_shape=(shap...]
  transfers between devices with their start and end apart: 0 -> 1, of which waited for: 0 -> 0; matrix products, arithmetic and copies ran while one was open for 0% -> 0% of each run, Pallas kernels for 0% -> 4%
where the time goes in v3:
time: 123 us
  Pallas kernels  121 us (98%)
  starting transfers between devices  1.6 us (1%)
    pallas_call x1, Pallas kernels, per_device(): pl.pallas_call(functools.partial(kernel, width, scale), out_shape=(pltpu....  114 us
    pallas_call x1, Pallas kernels, per_device(): pl.pallas_call(functools.partial(put_first, first, stop), out_shape=(shap...  5.05 us
  transfers between devices with their start and end apart: 1, of which 0 were waited for; matrix products, arithmetic and copies ran while one was open for 0% of the time, Pallas kernels for 4%

profile of v3, /device:TPU:102, one launch (start us, length us, event | category | flops | bytes accessed | tf_op | source)
XLA Modules:
  0.0 123.0 jit_solution(4550499279734688529)
XLA Ops:
  0.6 114.0 %shard_map.41 = (f32[8,128,16,128]{3,2,1,0:T(8,128)S(1)}, f32[8,128,16,128]{3,2,1,0:T(8,128)S(1)}, f32[5,8,8,128]{3,2,1,0:T(8,128)S(1)}, f32[5,8,8,128]{3,2,1,0:T(8,128)S(1)}) custom-call(f32[8,128,16,128]{3,2,1,0:T(8,128)} %field_hbm.1, f32[8,128,16,128]{3,2,1,0:T(8,128)} %crowd_hbm.1), custom_call_target="tpu_custom_call" | custom-call | tf_op jit(solution)/shard_map/pallas_call | solution.py:421
  114.7 1.6 %collective-permute-start = (f32[5,8,8,128]{3,2,1,0:T(8,128)S(1)}, f32[5,8,8,128]{3,2,1,0:T(8,128)S(1)}, u32[]{:S(2)}, u32[]{:S(2)}) collective-permute-start(f32[5,8,8,128]{3,2,1,0:T(8,128)S(1)} %get-tuple-element.10), channel_id=1, source_target_pairs={{0,1},{1,0},{2,3},{3,2},{4,5},{5,4},{6,7},{7,6},{8,9},{9,8},{10,11... | collective-permute-start | bytes 491528 | tf_op jit(solution)/shard_map/ppermute | solution.py:452
  116.3 5.1 %shard_map.42 = (f32[8,128,16,128]{3,2,1,0:T(8,128)}, f32[8,128,16,128]{3,2,1,0:T(8,128)}) custom-call(f32[8,128,16,128]{3,2,1,0:T(8,128)S(1)} %get-tuple-element.8.pot, f32[8,128,16,128]{3,2,1,0:T(8,128)S(1)} %get-tuple-element.11.end), custom_call_target="tpu_custom_call" | custom-call | bytes 16777216 | tf_op jit(solution)/shard_map/pallas_call | solution.py:454
  121.3 0.0 collective-permute-done.BL
  121.3 1.6 %shard_map.43 = f32[8,128,16,128]{3,2,1,0:T(8,128)} custom-call(f32[8,128,16,128]{3,2,1,0:T(8,128)S(1)} %get-tuple-element.8.pot, f32[5,8,8,128]{3,2,1,0:T(8,128)S(1)} %get-tuple-element.9.VL, f32[5,8,8,128]{3,2,1,0:T(8,128)S(1)} %collective-permute-done.BL, f32[8,128,16,128]{3,2,1,0:T(8,128)} %get-tuple-element.12.pot_in), custom_call_target="tpu_custom_call", output_to_operand_aliasing={{}: (3, {})} | custom-call | tf_op jit(solution)/shard_map/pallas_call | solution.py:463
Async XLA Ops:
  114.7 6.7 %collective-permute-start = (f32[5,8,8,128]{3,2,1,0:T(8,128)S(1)}, f32[5,8,8,128]{3,2,1,0:T(8,128)S(1)}, u32[]{:S(2)}, u32[]{:S(2)}) collective-permute-start(f32[5,8,8,128]{3,2,1,0:T(8,128)S(1)} %get-tuple-element.10), channel_id=1, source_target_pairs={{0,1},{1,0},{2,3},{3,2},{4,5},{5,4},{6,7},{7,6},{8,9},{9,8},{10,11... | collective-permute-start | bytes 491528 | tf_op jit(solution)/shard_map/ppermute | solution.py:452

commit v4 on v3

--- a/solution.py
+++ b/solution.py
@@ -11,8 +11,8 @@
 GROUP = 8
 FIRST = 2
 SECOND = 5
-LATE = 5
-DIRECT = 3
+LATE = 6
+DIRECT = 2
 MESH = pl.DeviceIdType.MESH
 
 
@@ -393,13 +393,15 @@
     ny = pot.shape[0]
     copies = []
     for k in range(LATE):
-        def row(y, carry, k=k):
-            below = (VL[k, y] + BL[k, y]) * scale
-            for j in range(width):
-                held[k, y, j] = pot[y, first + k * width + j] + below[j : j + 1]
+        def rows(turn, carry, k=k):
+            for part in range(4):
+                y = turn * 4 + part
+                below = (VL[k, y] + BL[k, y]) * scale
+                for j in range(width):
+                    held[k, y, j] = pot[y, first + k * width + j] + below[j : j + 1]
             return carry
 
-        lax.fori_loop(0, ny, row, 0)
+        lax.fori_loop(0, ny // 4, rows, 0)
         copies.append(
             pltpu.make_async_copy(held.at[k], pot_out.at[:, first + k * width : first + (k + 1) * width], sems.at[k])
         )

time: 123 us -> 123 us (level)
  no operation moved by 1% of the time
where the time goes in v4:
time: 123 us
  Pallas kernels  121 us (98%)
  starting transfers between devices  1.46 us (1%)
    pallas_call x1, Pallas kernels, per_device(): pl.pallas_call(functools.partial(kernel, width, scale), out_shape=(pltpu....  114 us
    pallas_call x1, Pallas kernels, per_device(): pl.pallas_call(functools.partial(put_first, first, stop), out_shape=(shap...  4.89 us
  transfers between devices with their start and end apart: 1, of which 0 were waited for; matrix products, arithmetic and copies ran while one was open for 0% of the time, Pallas kernels for 4%

profile of v4, /device:TPU:102, one launch (start us, length us, event | category | flops | bytes accessed | tf_op | source)
XLA Modules:
  0.0 122.7 jit_solution(14221330814941154437)
XLA Ops:
  0.6 113.9 %shard_map.41 = (f32[8,128,16,128]{3,2,1,0:T(8,128)S(1)}, f32[8,128,16,128]{3,2,1,0:T(8,128)S(1)}, f32[6,8,8,128]{3,2,1,0:T(8,128)S(1)}, f32[6,8,8,128]{3,2,1,0:T(8,128)S(1)}) custom-call(f32[8,128,16,128]{3,2,1,0:T(8,128)} %field_hbm.1, f32[8,128,16,128]{3,2,1,0:T(8,128)} %crowd_hbm.1), custom_call_target="tpu_custom_call" | custom-call | tf_op jit(solution)/shard_map/pallas_call | solution.py:423
  114.6 1.5 %collective-permute-start = (f32[6,8,8,128]{3,2,1,0:T(8,128)S(1)}, f32[6,8,8,128]{3,2,1,0:T(8,128)S(1)}, u32[]{:S(2)}, u32[]{:S(2)}) collective-permute-start(f32[6,8,8,128]{3,2,1,0:T(8,128)S(1)} %get-tuple-element.10), channel_id=1, source_target_pairs={{0,1},{1,0},{2,3},{3,2},{4,5},{5,4},{6,7},{7,6},{8,9},{9,8},{10,11... | collective-permute-start | bytes 589832 | tf_op jit(solution)/shard_map/ppermute | solution.py:454
  116.0 4.9 %shard_map.42 = (f32[8,128,16,128]{3,2,1,0:T(8,128)}, f32[8,128,16,128]{3,2,1,0:T(8,128)}) custom-call(f32[8,128,16,128]{3,2,1,0:T(8,128)S(1)} %get-tuple-element.8.pot, f32[8,128,16,128]{3,2,1,0:T(8,128)S(1)} %get-tuple-element.11.end), custom_call_target="tpu_custom_call" | custom-call | bytes 16777216 | tf_op jit(solution)/shard_map/pallas_call | solution.py:456
  120.9 0.0 collective-permute-done.BL
  120.9 1.8 %shard_map.43 = f32[8,128,16,128]{3,2,1,0:T(8,128)} custom-call(f32[8,128,16,128]{3,2,1,0:T(8,128)S(1)} %get-tuple-element.8.pot, f32[6,8,8,128]{3,2,1,0:T(8,128)S(1)} %get-tuple-element.9.VL, f32[6,8,8,128]{3,2,1,0:T(8,128)S(1)} %collective-permute-done.BL, f32[8,128,16,128]{3,2,1,0:T(8,128)} %get-tuple-element.12.pot_in), custom_call_target="tpu_custom_call", output_to_operand_aliasing={{}: (3, {})} | custom-call | tf_op jit(solution)/shard_map/pallas_call | solution.py:465
Async XLA Ops:
  114.6 6.4 %collective-permute-start = (f32[6,8,8,128]{3,2,1,0:T(8,128)S(1)}, f32[6,8,8,128]{3,2,1,0:T(8,128)S(1)}, u32[]{:S(2)}, u32[]{:S(2)}) collective-permute-start(f32[6,8,8,128]{3,2,1,0:T(8,128)S(1)} %get-tuple-element.10), channel_id=1, source_target_pairs={{0,1},{1,0},{2,3},{3,2},{4,5},{5,4},{6,7},{7,6},{8,9},{9,8},{10,11... | collective-permute-start | bytes 589832 | tf_op jit(solution)/shard_map/ppermute | solution.py:454
